TPU v7x, 32 devices: a whole 2x2x4 slice. The times are simulated.
32 devices in a mesh: seq: 8 (over y, x, core), dp: 4 (over z).
Axes of the slice: x: 2, y: 2, z: 4, core: 2. Of those that a mesh axis runs over, the one named last changes fastest.
Arguments:
- teacher_video: bfloat16 [4, 3, 1024, 1536], P('dp', None, 'seq'), may hold values from -150 to 150
- student_video: bfloat16 [4, 3, 1024, 1536], P('dp', None, 'seq'), may hold values from -150 to 150
- teacher_audio: bfloat16 [4, 2, 256, 1536], P('dp', None, 'seq'), may hold values from -5 to 5
- student_audio: bfloat16 [4, 2, 256, 1536], P('dp', None, 'seq'), may hold values from -5 to 5
- alignment: int32 [4, 8, 2], P('dp', 'seq'), may hold values from 0 to 7, as said below
- guidance_index: int32 [4], P('dp'), may hold values from 0 to 7
- step_index: int32 [4], P('dp'), may hold values from 0 to 999
- null_flag: int32 [4], P('dp'), may hold values from 0 to 1, as said below
- gamma: float32 [8, 12], replicated, may hold values from -0.5 to 0.5
Outputs:
- grad_video: bfloat16 [4, 3, 1024, 1536], P('dp', None, 'seq')
- grad_audio: bfloat16 [4, 2, 256, 1536], P('dp', None, 'seq')
- gamma_grad: float32 [8, 12], replicated
Inputs may be any that keep to these rules, and one draw needn't show every extreme that they name: For video block i, alignment[b, i] holds the first audio block s and the number c >= 1 of consecutive audio blocks that intersect it in time; blocks s to s + c - 1 lie inside the clip and within 3 blocks of audio block i. `null_flag`: at least one clip is dropped and at least one is kept.
All inputs are finite; a program needn't handle non-finite values.
Results may differ from a plain program's by a relative error of at most 0.013.
Values may be sent and summed in bfloat16 or wider, within the bound.
A program may use at most 64 MiB of HBM per device.

v0:
```python
import jax
import jax.numpy as jnp
from jax import lax
from jax.sharding import PartitionSpec as P

VB = 128
REACH = 3


def from_behind(x, axis, by):
    peers = lax.axis_size(axis)
    pairs = [(i, i + by) for i in range(peers) if 0 <= i + by < peers]
    return lax.ppermute(x, axis, pairs)


def joint_probs(scores, usable):
    masked = jnp.where(usable, scores, -jnp.inf)
    highest = jnp.max(masked, axis=-1, keepdims=True)
    exponent = jnp.exp(masked - highest)
    return exponent / jnp.sum(exponent, axis=-1, keepdims=True)


def body(
    teacher_video,
    student_video,
    teacher_audio,
    student_audio,
    alignment,
    guidance_index,
    step_index,
    null_flag,
    gamma,
):
    reach_blocks = REACH
    head_count = gamma.shape[1]
    feature_width = teacher_video.shape[-1]
    head_dim = feature_width // head_count
    tokens = teacher_video.shape[2]
    audio_tokens = teacher_audio.shape[2]
    blocks = tokens // VB
    window = (2 * reach_blocks + 1) * audio_tokens
    score_scale = head_dim ** (-0.5)
    position = lax.axis_index("seq")
    level_index = guidance_index[0]
    weight = 1.0 + 0.75 * level_index.astype(jnp.float32)
    loss_weight = 1.0 / (1.0 + step_index[0].astype(jnp.float32) / 250.0)
    keep_audio = null_flag[0] == 0
    levels = jnp.arange(gamma.shape[0], dtype=jnp.int32)
    factor = jnp.sum(
        jnp.where(levels[:, None] == level_index, gamma, jnp.zeros_like(gamma)), axis=0
    )
    own_audio = (teacher_audio[0], student_audio[0])
    above = []
    carried = own_audio
    for hop in range(reach_blocks):
        carried = from_behind((carried[0], carried[1]), "seq", -1)
        above.append(carried)
    below = []
    carried = own_audio
    for hop in range(reach_blocks):
        carried = from_behind((carried[0], carried[1]), "seq", 1)
        below.append(carried)
    pieces = below[::-1] + [own_audio] + above
    teach_window = jnp.concatenate([piece[0] for piece in pieces], axis=1).reshape(
        2, window, head_count, head_dim
    )
    pupil_window = jnp.concatenate([piece[1] for piece in pieces], axis=1).reshape(
        2, window, head_count, head_dim
    )
    owners = position - reach_blocks + jnp.arange(window, dtype=jnp.int32) // audio_tokens
    teach_vid = teacher_video[0].reshape(3, blocks, VB, head_count, head_dim)
    pupil_vid = student_video[0].reshape(3, blocks, VB, head_count, head_dim)
    audio_sums = jnp.zeros((2, window, feature_width), jnp.float32)
    first_block = alignment[0, 0, 0]
    block_count = alignment[0, 0, 1]
    audio_ok = (owners >= first_block) & (owners < first_block + block_count) & keep_audio
    usable = jnp.concatenate([jnp.ones((VB,), bool), audio_ok])[None, None, :]
    teach_keys = jnp.concatenate([teach_vid[1, 0], teach_window[0]], axis=0)
    teach_values = jnp.concatenate([teach_vid[2, 0], teach_window[1]], axis=0)
    teach_scores = (
        jnp.einsum("qhe,khe->hqk", teach_vid[0, 0], teach_keys, preferred_element_type=jnp.float32)
        * score_scale
    )
    cond_probs = joint_probs(teach_scores, usable).astype(jnp.bfloat16)
    conditional = jnp.einsum(
        "hqk,khe->qhe", cond_probs, teach_values, preferred_element_type=jnp.float32
    )
    plain_probs = joint_probs(teach_scores[..., :VB], jnp.ones((1, 1, VB), bool)).astype(
        jnp.bfloat16
    )
    unconditional = jnp.einsum(
        "hqk,khe->qhe", plain_probs, teach_vid[2, 0], preferred_element_type=jnp.float32
    )
    target = unconditional + weight * (conditional - unconditional)
    pupil_query = pupil_vid[0, 0]
    pupil_keys = jnp.concatenate([pupil_vid[1, 0], pupil_window[0]], axis=0)
    pupil_values = jnp.concatenate([pupil_vid[2, 0], pupil_window[1]], axis=0)
    pupil_scores = (
        jnp.einsum("qhe,khe->hqk", pupil_query, pupil_keys, preferred_element_type=jnp.float32)
        * score_scale
    )
    probs = joint_probs(pupil_scores, usable)
    probs_round = probs.astype(jnp.bfloat16)
    student_out = jnp.einsum(
        "hqk,khe->qhe", probs_round, pupil_values, preferred_element_type=jnp.float32
    )
    residual = loss_weight * (student_out * factor[None, :, None] - target)
    head_totals = jnp.sum(residual * student_out, axis=(0, 2))
    out_grad = (residual * factor[None, :, None]).astype(jnp.bfloat16)
    prob_grad = jnp.einsum(
        "qhe,khe->hqk", out_grad, pupil_values, preferred_element_type=jnp.float32
    )
    row_delta = jnp.sum(out_grad.astype(jnp.float32) * student_out, axis=-1)
    score_grad = (score_scale * probs * (prob_grad - jnp.transpose(row_delta)[:, :, None])).astype(
        jnp.bfloat16
    )
    query_grad = jnp.einsum(
        "hqk,khe->qhe", score_grad, pupil_keys, preferred_element_type=jnp.float32
    )
    key_grad = jnp.einsum(
        "hqk,qhe->khe", score_grad, pupil_query, preferred_element_type=jnp.float32
    )
    value_grad = jnp.einsum(
        "hqk,qhe->khe", probs_round, out_grad, preferred_element_type=jnp.float32
    )
    video_blocks = [
        jnp.stack([query_grad, key_grad[:VB], value_grad[:VB]])
        .reshape(3, VB, feature_width)
        .astype(jnp.bfloat16)
    ]
    audio_sums = jnp.stack([key_grad[VB:], value_grad[VB:]]).reshape(2, window, feature_width)

    def slot_piece(offset):
        begin = (offset + reach_blocks) * audio_tokens
        return audio_sums[:, begin : begin + audio_tokens]

    own_total = slot_piece(0)
    collected = jnp.zeros_like(own_total)
    for offset in range(reach_blocks, 0, -1):
        collected = from_behind(collected + slot_piece(offset), "seq", 1)
    gathered_low = jnp.zeros_like(own_total)
    for offset in range(-reach_blocks, 0):
        gathered_low = from_behind(gathered_low + slot_piece(offset), "seq", -1)
    own_total = own_total + collected + gathered_low
    grad_audio = own_total.astype(jnp.bfloat16)[None]
    grad_video = jnp.stack(video_blocks, axis=1).reshape(3, tokens, feature_width)[None]
    total_tokens = tokens * lax.axis_size("seq")
    contribution = jnp.where(
        levels[:, None] == level_index, head_totals[None, :], jnp.zeros_like(gamma)
    ) / (total_tokens * head_dim)
    gamma_grad = lax.psum(contribution, ("seq", "dp"))
    return (grad_video, grad_audio, gamma_grad)


def solution(mesh):
    return jax.shard_map(
        body,
        mesh=mesh,
        in_specs=(
            P("dp", None, "seq", None),
            P("dp", None, "seq", None),
            P("dp", None, "seq", None),
            P("dp", None, "seq", None),
            P("dp", "seq", None),
            P("dp"),
            P("dp"),
            P("dp"),
            P(),
        ),
        out_specs=(P("dp", None, "seq", None), P("dp", None, "seq", None), P()),
        check_vma=False,
    )
```

profile of v0, /device:TPU:0, one launch (start us, length us, event | category | flops | bytes accessed | tf_op | source)
XLA Modules:
  0.0 180.7 jit_solution(4961280684890227029)
XLA Ops:
  0.6 1.4 collective-permute-start.9
  2.1 3.0 %collective-permute-start.6 = (bf16[2,32,1536]{2,1,0:T(8,128)(2,1)}, bf16[2,32,1536]{2,1,0:T(8,128)(2,1)S(1)}, u32[]{:S(2)}, u32[]{:S(2)}) collective-permute-start(bf16[2,32,1536]{2,1,0:T(8,128)(2,1)} %bitcast.108), channel_id=1, source_target_pairs={{0,4},{4,8},{8,12},{12,16},{16,20},{20,24},{24,28},{1,5},{5,9},{9,... | collective-permute-start | bytes 589832 | tf_op jit(solution)/shard_map/ppermute | solution.py:13
  5.1 1.3 collective-permute-start.3
  6.4 5.8 %collective-permute-start = (bf16[2,32,1536]{2,1,0:T(8,128)(2,1)}, bf16[2,32,1536]{2,1,0:T(8,128)(2,1)}, u32[]{:S(2)}, u32[]{:S(2)}) collective-permute-start(bf16[2,32,1536]{2,1,0:T(8,128)(2,1)} %bitcast.106), channel_id=1, source_target_pairs={{0,4},{4,8},{8,12},{12,16},{16,20},{20,24},{24,28},{1,5},{5,9},{9,... | collective-permute-start | bytes 589832 | tf_op jit(solution)/shard_map/ppermute | solution.py:13
  12.2 1.3 fusion.85
  19.1 0.9 copy.92
  21.4 3.0 %collective-permute-start.1 = (bf16[2,32,1536]{2,1,0:T(8,128)(2,1)}, bf16[2,32,1536]{2,1,0:T(8,128)(2,1)S(1)}, u32[]{:S(2)}, u32[]{:S(2)}) collective-permute-start(bf16[2,32,1536]{2,1,0:T(8,128)(2,1)} %collective-permute-done), channel_id=1, source_target_pairs={{0,4},{4,8},{8,12},{12,16},{16,20},{20,24},{24,28},{1,5},{5,9},{9,... | collective-permute-start | bytes 589832 | tf_op jit(solution)/shard_map/ppermute | solution.py:13
  27.0 1.3 collective-permute-start.10
  28.3 3.3 %collective-permute-start.7 = (bf16[2,32,1536]{2,1,0:T(8,128)(2,1)S(1)}, bf16[2,32,1536]{2,1,0:T(8,128)(2,1)S(1)}, u32[]{:S(2)}, u32[]{:S(2)}) collective-permute-start(bf16[2,32,1536]{2,1,0:T(8,128)(2,1)S(1)} %collective-permute-done.6), channel_id=1, source_target_pairs={{0,4},{4,8},{8,12},{12,16},{16,20},{20,24},{24,28},{1,5},{5,9},{9,... | collective-permute-start | bytes 589832 | tf_op jit(solution)/shard_map/ppermute | solution.py:13
  31.6 1.3 collective-permute-start.4
  32.9 5.2 %collective-permute-start.2 = (bf16[2,32,1536]{2,1,0:T(8,128)(2,1)S(1)}, bf16[2,32,1536]{2,1,0:T(8,128)(2,1)S(1)}, u32[]{:S(2)}, u32[]{:S(2)}) collective-permute-start(bf16[2,32,1536]{2,1,0:T(8,128)(2,1)S(1)} %collective-permute-done.1), channel_id=1, source_target_pairs={{0,4},{4,8},{8,12},{12,16},{16,20},{20,24},{24,28},{1,5},{5,9},{9,... | collective-permute-start | bytes 589832 | tf_op jit(solution)/shard_map/ppermute | solution.py:13
  38.2 1.3 collective-permute-start.11
  39.5 4.9 %collective-permute-start.8 = (bf16[2,32,1536]{2,1,0:T(8,128)(2,1)S(1)}, bf16[2,32,1536]{2,1,0:T(8,128)(2,1)}, u32[]{:S(2)}, u32[]{:S(2)}) collective-permute-start(bf16[2,32,1536]{2,1,0:T(8,128)(2,1)S(1)} %collective-permute-done.7), channel_id=1, source_target_pairs={{0,4},{4,8},{8,12},{12,16},{16,20},{20,24},{24,28},{1,5},{5,9},{9,... | collective-permute-start | bytes 589832 | tf_op jit(solution)/shard_map/ppermute | solution.py:13
  44.4 1.5 collective-permute-start.5
  46.0 0.9 constant_dynamic-update-slice_fusion.4
  46.9 0.9 constant_dynamic-update-slice_fusion.2
  49.4 1.1 copy.99
  50.5 0.9 constant_dynamic-update-slice_fusion.13
  52.0 1.2 copy.110
  54.3 1.8 multiply_bitcast_fusion
  56.9 1.3 fusion.87
  58.2 2.4 %convolution_bitcast_fusion.2 = f32[128,12,128]{0,2,1:T(8,128)} fusion(bf16[128,12,128]{0,2,1:T(8,128)(2,1)S(1)} %bitcast.98, f32[12,128]{1,0:T(8,128)S(1)} %fusion.87, f32[12,128,352]{1,2,0:T(8,128)} %multiply_bitcast_fusion), kind=kOutput, calls=%fused_computation.30 | convolution fusion | flops 50923136 | bytes 1972224 | tf_op jit(solution)/shard_map/hqk,khe->qhe/dot_general | solution.py:91
  62.3 1.5 convolution_bitcast_fusion.4
  63.7 3.7 %multiply_reduce_fusion = (f32[12]{0:T(128)S(1)}, f32[128,12]{0,1:T(8,128)S(1)}, bf16[128,12,128]{0,2,1:T(8,128)(2,1)}) fusion(f32[128,12,128]{0,2,1:T(8,128)} %convolution_bitcast_fusion.4, f32[12]{0:T(128)S(1)} %select_reduce_fusion.1, f32[128,12,128]{0,2,1:T(8,128)} %convolution_bitcast_fusion.2, f32[12,128]{1,0:T(8,128)S(1)} %fusion.88, ...), kind=kOutput, calls=%fused_computation.57 | convolution fusion | flops 286409056 | bytes 4534728 | tf_op jit(solution)/shard_map/hqk,khe->qhe/dot_general | solution.py:85
  67.4 2.3 %convolution_bitcast_fusion = f32[352,12,128]{2,0,1:T(8,128)S(1)} fusion(bf16[128,12,128]{0,2,1:T(8,128)(2,1)} %get-tuple-element.14, f32[12,128,352]{1,2,0:T(8,128)} %copy-done.20, f32[12,128]{1,0:T(8,128)S(1)} %get-tuple-element.29), kind=kOutput, calls=%fused_computation.26 | convolution fusion | flops 139493376 | bytes 4724736 | tf_op jit(solution)/shard_map/hqk,qhe->khe/dot_general | solution.py:123
  69.9 1.6 multiply_convert_fusion
  72.5 1.7 convolution_bitcast_fusion.1
  74.2 1.3 copy-done
  75.7 1.7 copy.116
  77.3 1.9 %copy.118 = f32[1,224,1536]{2,1,0:T(8,128)S(1)} copy(f32[1,224,1536]{1,2,0:T(8,128)} %bitcast.87) | data formatting | bytes 2752512 | tf_op jit(solution)/shard_map/stack | solution.py:131
  79.2 8.3 %collective-permute-start.12 = (f32[2,32,1536]{2,1,0:T(8,128)S(1)}, f32[2,32,1536]{2,1,0:T(8,128)S(1)}, u32[]{:S(2)}, u32[]{:S(2)}) collective-permute-start(f32[2,32,1536]{2,1,0:T(8,128)S(1)} %fusion.35), channel_id=1, source_target_pairs={{0,4},{4,8},{8,12},{12,16},{16,20},{20,24},{24,28},{1,5},{5,9},{9,... | collective-permute-start | bytes 1179656 | tf_op jit(solution)/shard_map/ppermute | solution.py:13
  87.5 1.3 collective-permute-done.12
  88.9 5.3 %collective-permute-start.13 = (f32[2,32,1536]{2,1,0:T(8,128)S(1)}, f32[2,32,1536]{2,1,0:T(8,128)S(1)}, u32[]{:S(2)}, u32[]{:S(2)}) collective-permute-start(f32[2,32,1536]{2,1,0:T(8,128)S(1)} %fusion.37), channel_id=1, source_target_pairs={{0,4},{4,8},{8,12},{12,16},{16,20},{20,24},{24,28},{1,5},{5,9},{9,... | collective-permute-start | bytes 1179656 | tf_op jit(solution)/shard_map/ppermute | solution.py:13
  94.2 1.3 collective-permute-done.13
  96.3 1.3 collective-permute-start.15
  97.6 7.7 %collective-permute-done.15 = f32[2,32,1536]{2,1,0:T(8,128)S(1)} collective-permute-done((f32[2,32,1536]{2,1,0:T(8,128)S(1)}, f32[2,32,1536]{2,1,0:T(8,128)S(1)}, u32[]{:S(2)}, u32[]{:S(2)}) %collective-permute-start.15) | collective-permute-done | bytes 393248 | tf_op jit(solution)/shard_map/ppermute | solution.py:13
  106.1 1.3 collective-permute-start.16
  107.4 2.0 %slice.191 = bf16[128,12,128]{2,0,1:T(8,128)(2,1)} slice(f32[352,12,128]{2,0,1:T(8,128)} %copy-done.10), slice={[0:128], [0:12], [0:128]} | slice | bytes 786432 | tf_op jit(solution)/shard_map/slice | solution.py:127
  109.3 2.0 %slice.192 = bf16[128,12,128]{2,0,1:T(8,128)(2,1)} slice(f32[352,12,128]{2,0,1:T(8,128)} %copy-done), slice={[0:128], [0:12], [0:128]} | slice | bytes 786432 | tf_op jit(solution)/shard_map/slice | solution.py:127
  111.4 1.9 %copy.115 = bf16[128,12,128]{0,2,1:T(8,128)(2,1)} copy(bf16[128,12,128]{2,0,1:T(8,128)(2,1)} %slice.191) | data formatting | bytes 786432 | tf_op jit(solution)/shard_map/slice | solution.py:127
  113.3 1.9 %copy.113 = bf16[128,12,128]{0,2,1:T(8,128)(2,1)} copy(bf16[128,12,128]{2,0,1:T(8,128)(2,1)} %slice.192) | data formatting | bytes 786432 | tf_op jit(solution)/shard_map/slice | solution.py:127
  115.2 1.9 %convolution_convert_fusion = bf16[12,128,128]{2,1,0:T(8,128)(2,1)S(1)} fusion(bf16[12,128,352]{1,2,0:T(8,128)(2,1)} %multiply_convert_fusion, bf16[224,12,128]{2,0,1:T(8,128)(2,1)S(1)} %copy-done.2, bf16[128,12,128]{2,0,1:T(8,128)(2,1)} %copy.92), kind=kOutput, calls=%fused_computation.38 | convolution fusion | flops 140771328 | bytes 2555904 | tf_op jit(solution)/shard_map/hqk,khe->qhe/dot_general | solution.py:117
  117.1 9.4 %collective-permute-start.14 = (f32[2,32,1536]{2,1,0:T(8,128)}, f32[2,32,1536]{2,1,0:T(8,128)S(1)}, u32[]{:S(2)}, u32[]{:S(2)}) collective-permute-start(f32[2,32,1536]{2,1,0:T(8,128)} %get-tuple-element.15), channel_id=1, source_target_pairs={{0,4},{4,8},{8,12},{12,16},{16,20},{20,24},{24,28},{1,5},{5,9},{9,... | collective-permute-start | bytes 1179656 | tf_op jit(solution)/shard_map/ppermute | solution.py:13
  126.6 1.8 fusion.41
  128.3 1.3 collective-permute-start.17
  129.7 1.2 pad_maximum_fusion
  130.8 2.4 %copy.120 = bf16[1,3,128,1536]{3,2,1,0:T(8,128)(2,1)} copy(bf16[1,3,128,1536]{2,3,1,0:T(8,128)(2,1)} %pad_maximum_fusion) | data formatting | bytes 2359296
  133.3 46.7 %psum.7 = f32[8,12]{1,0:T(8,128)} all-reduce(f32[8,12]{1,0:T(8,128)S(1)} %select_multiply_fusion), channel_id=1, replica_groups=mesh['seq'=8,'dp'=4] {'seq','dp'}, use_global_device_ids=true, to_apply=%region_9.10 | all-reduce | flops 96 | bytes 768 | tf_op jit(solution)/shard_map/psum | solution.py:151
  (107 shorter events, 15.6 us)
Async XLA Ops:
  0.6 12.9 %copy-start.11 = (bf16[1,3,128,1536]{3,2,1,0:T(8,128)(2,1)S(1)}, bf16[1,3,128,1536]{3,2,1,0:T(8,128)(2,1)}, u32[]{:S(2)}) copy-start(bf16[1,3,128,1536]{3,2,1,0:T(8,128)(2,1)} %param.10) | copy-start | bytes 3538948
  0.6 26.3 %collective-permute-start.9 = (bf16[2,32,1536]{2,1,0:T(8,128)(2,1)}, bf16[2,32,1536]{2,1,0:T(8,128)(2,1)S(1)}, u32[]{:S(2)}, u32[]{:S(2)}) collective-permute-start(bf16[2,32,1536]{2,1,0:T(8,128)(2,1)} %bitcast.107), channel_id=1, source_target_pairs={{4,0},{8,4},{12,8},{16,12},{20,16},{24,20},{28,24},{5,1},{9,5},{13... | collective-permute-start | bytes 589832 | tf_op jit(solution)/shard_map/ppermute | solution.py:13
  2.1 26.2 %collective-permute-start.6 = (bf16[2,32,1536]{2,1,0:T(8,128)(2,1)}, bf16[2,32,1536]{2,1,0:T(8,128)(2,1)S(1)}, u32[]{:S(2)}, u32[]{:S(2)}) collective-permute-start(bf16[2,32,1536]{2,1,0:T(8,128)(2,1)} %bitcast.108), channel_id=1, source_target_pairs={{0,4},{4,8},{8,12},{12,16},{16,20},{20,24},{24,28},{1,5},{5,9},{9,... | collective-permute-start | bytes 589832 | tf_op jit(solution)/shard_map/ppermute | solution.py:13
  5.1 26.5 %collective-permute-start.3 = (bf16[2,32,1536]{2,1,0:T(8,128)(2,1)}, bf16[2,32,1536]{2,1,0:T(8,128)(2,1)}, u32[]{:S(2)}, u32[]{:S(2)}) collective-permute-start(bf16[2,32,1536]{2,1,0:T(8,128)(2,1)} %bitcast.105), channel_id=1, source_target_pairs={{4,0},{8,4},{12,8},{16,12},{20,16},{24,20},{28,24},{5,1},{9,5},{13... | collective-permute-start | bytes 589832 | tf_op jit(solution)/shard_map/ppermute | solution.py:13
  6.4 15.0 %collective-permute-start = (bf16[2,32,1536]{2,1,0:T(8,128)(2,1)}, bf16[2,32,1536]{2,1,0:T(8,128)(2,1)}, u32[]{:S(2)}, u32[]{:S(2)}) collective-permute-start(bf16[2,32,1536]{2,1,0:T(8,128)(2,1)} %bitcast.106), channel_id=1, source_target_pairs={{0,4},{4,8},{8,12},{12,16},{16,20},{20,24},{24,28},{1,5},{5,9},{9,... | collective-permute-start | bytes 589832 | tf_op jit(solution)/shard_map/ppermute | solution.py:13
  17.0 3.0 %copy-start.6 = (bf16[1,1,128,1536]{2,3,1,0:T(8,128)(2,1)}, bf16[1,1,128,1536]{2,3,1,0:T(8,128)(2,1)S(1)}, u32[]{:S(2)}) copy-start(bf16[1,1,128,1536]{2,3,1,0:T(8,128)(2,1)S(1)} %copy.106) | copy-start | bytes 1179652
  20.0 4.4 %copy-start.19 = (s32[1,1,2]{2,1,0:T(1,128)S(1)}, s32[1,1,2]{2,1,0:T(1,128)}, u32[]{:S(2)}) copy-start(s32[1,1,2]{2,1,0:T(1,128)} %param.13) | copy-start | bytes 28
  20.0 18.1 %copy-start.18 = (f32[8,12]{1,0:T(8,128)S(1)}, f32[8,12]{1,0:T(8,128)}, u32[]{:S(2)}) copy-start(f32[8,12]{1,0:T(8,128)} %param.17) | copy-start | bytes 1156
  20.2 26.7 %copy-start.16 = (bf16[1,2,32,1536]{3,2,1,0:T(8,128)(2,1)S(1)}, bf16[1,2,32,1536]{3,2,1,0:T(8,128)(2,1)}, u32[]{:S(2)}) copy-start(bf16[1,2,32,1536]{3,2,1,0:T(8,128)(2,1)} %param.12) | copy-start | bytes 589828
  21.4 11.5 %collective-permute-start.1 = (bf16[2,32,1536]{2,1,0:T(8,128)(2,1)}, bf16[2,32,1536]{2,1,0:T(8,128)(2,1)S(1)}, u32[]{:S(2)}, u32[]{:S(2)}) collective-permute-start(bf16[2,32,1536]{2,1,0:T(8,128)(2,1)} %collective-permute-done), channel_id=1, source_target_pairs={{0,4},{4,8},{8,12},{12,16},{16,20},{20,24},{24,28},{1,5},{5,9},{9,... | collective-permute-start | bytes 589832 | tf_op jit(solution)/shard_map/ppermute | solution.py:13
  27.0 11.2 %collective-permute-start.10 = (bf16[2,32,1536]{2,1,0:T(8,128)(2,1)S(1)}, bf16[2,32,1536]{2,1,0:T(8,128)(2,1)S(1)}, u32[]{:S(2)}, u32[]{:S(2)}) collective-permute-start(bf16[2,32,1536]{2,1,0:T(8,128)(2,1)S(1)} %collective-permute-done.9), channel_id=1, source_target_pairs={{4,0},{8,4},{12,8},{16,12},{20,16},{24,20},{28,24},{5,1},{9,5},{13... | collective-permute-start | bytes 589832 | tf_op jit(solution)/shard_map/ppermute | solution.py:13
  28.3 11.2 %collective-permute-start.7 = (bf16[2,32,1536]{2,1,0:T(8,128)(2,1)S(1)}, bf16[2,32,1536]{2,1,0:T(8,128)(2,1)S(1)}, u32[]{:S(2)}, u32[]{:S(2)}) collective-permute-start(bf16[2,32,1536]{2,1,0:T(8,128)(2,1)S(1)} %collective-permute-done.6), channel_id=1, source_target_pairs={{0,4},{4,8},{8,12},{12,16},{16,20},{20,24},{24,28},{1,5},{5,9},{9,... | collective-permute-start | bytes 589832 | tf_op jit(solution)/shard_map/ppermute | solution.py:13
  31.6 12.9 %collective-permute-start.4 = (bf16[2,32,1536]{2,1,0:T(8,128)(2,1)}, bf16[2,32,1536]{2,1,0:T(8,128)(2,1)S(1)}, u32[]{:S(2)}, u32[]{:S(2)}) collective-permute-start(bf16[2,32,1536]{2,1,0:T(8,128)(2,1)} %collective-permute-done.3), channel_id=1, source_target_pairs={{4,0},{8,4},{12,8},{16,12},{20,16},{24,20},{28,24},{5,1},{9,5},{13... | collective-permute-start | bytes 589832 | tf_op jit(solution)/shard_map/ppermute | solution.py:13
  32.9 13.0 %collective-permute-start.2 = (bf16[2,32,1536]{2,1,0:T(8,128)(2,1)S(1)}, bf16[2,32,1536]{2,1,0:T(8,128)(2,1)S(1)}, u32[]{:S(2)}, u32[]{:S(2)}) collective-permute-start(bf16[2,32,1536]{2,1,0:T(8,128)(2,1)S(1)} %collective-permute-done.1), channel_id=1, source_target_pairs={{0,4},{4,8},{8,12},{12,16},{16,20},{20,24},{24,28},{1,5},{5,9},{9,... | collective-permute-start | bytes 589832 | tf_op jit(solution)/shard_map/ppermute | solution.py:13
  38.2 13.4 %collective-permute-start.11 = (bf16[2,32,1536]{2,1,0:T(8,128)(2,1)S(1)}, bf16[2,32,1536]{2,1,0:T(8,128)(2,1)S(1)}, u32[]{:S(2)}, u32[]{:S(2)}) collective-permute-start(bf16[2,32,1536]{2,1,0:T(8,128)(2,1)S(1)} %collective-permute-done.10), channel_id=1, source_target_pairs={{4,0},{8,4},{12,8},{16,12},{20,16},{24,20},{28,24},{5,1},{9,5},{13... | collective-permute-start | bytes 589832 | tf_op jit(solution)/shard_map/ppermute | solution.py:13
  39.5 11.0 %collective-permute-start.8 = (bf16[2,32,1536]{2,1,0:T(8,128)(2,1)S(1)}, bf16[2,32,1536]{2,1,0:T(8,128)(2,1)}, u32[]{:S(2)}, u32[]{:S(2)}) collective-permute-start(bf16[2,32,1536]{2,1,0:T(8,128)(2,1)S(1)} %collective-permute-done.7), channel_id=1, source_target_pairs={{0,4},{4,8},{8,12},{12,16},{16,20},{20,24},{24,28},{1,5},{5,9},{9,... | collective-permute-start | bytes 589832 | tf_op jit(solution)/shard_map/ppermute | solution.py:13
  44.4 3.9 %collective-permute-start.5 = (bf16[2,32,1536]{2,1,0:T(8,128)(2,1)S(1)}, bf16[2,32,1536]{2,1,0:T(8,128)(2,1)S(1)}, u32[]{:S(2)}, u32[]{:S(2)}) collective-permute-start(bf16[2,32,1536]{2,1,0:T(8,128)(2,1)S(1)} %collective-permute-done.4), channel_id=1, source_target_pairs={{4,0},{8,4},{12,8},{16,12},{20,16},{24,20},{28,24},{5,1},{9,5},{13... | collective-permute-start | bytes 589832 | tf_op jit(solution)/shard_map/ppermute | solution.py:13
  49.1 11.5 %copy-start.1 = (bf16[224,12,128]{2,0,1:T(8,128)(2,1)}, bf16[224,12,128]{2,0,1:T(8,128)(2,1)S(1)}, u32[]{:S(2)}) copy-start(bf16[224,12,128]{2,0,1:T(8,128)(2,1)S(1)} %copy.93) | copy-start | bytes 2064388
  49.4 2.1 %copy-start.17 = (bf16[1,2,32,1536]{3,2,1,0:T(8,128)(2,1)S(1)}, bf16[1,2,32,1536]{3,2,1,0:T(8,128)(2,1)}, u32[]{:S(2)}) copy-start(bf16[1,2,32,1536]{3,2,1,0:T(8,128)(2,1)} %param.11) | copy-start | bytes 589828
  53.1 1.0 copy-start.4
  53.1 1.1 copy-start.5
  56.1 2.1 %copy-start.7 = (bf16[1,1,128,1536]{2,3,1,0:T(8,128)(2,1)S(1)}, bf16[1,1,128,1536]{2,3,1,0:T(8,128)(2,1)}, u32[]{:S(2)}) copy-start(bf16[1,1,128,1536]{2,3,1,0:T(8,128)(2,1)} %copy-done.6) | copy-start | bytes 1179652
  58.2 2.4 %copy-start.3 = (bf16[128,12,128]{2,0,1:T(8,128)(2,1)S(1)}, bf16[128,12,128]{2,0,1:T(8,128)(2,1)}, u32[]{:S(2)}) copy-start(bf16[128,12,128]{2,0,1:T(8,128)(2,1)} %copy.92) | copy-start | bytes 1179652
  61.0 1.1 copy-start.12
  61.1 1.2 copy-start.14
  61.8 1.9 %copy-start.20 = (f32[12,128,352]{1,2,0:T(8,128)}, f32[12,128,352]{1,2,0:T(8,128)S(1)}, u32[]{:S(2)}) copy-start(f32[12,128,352]{1,2,0:T(8,128)S(1)} %get-tuple-element.30) | copy-start | bytes 6488068
  62.3 1.5 copy-start.13
  67.4 2.3 %copy-start.15 = (bf16[128,12,128]{2,0,1:T(8,128)(2,1)S(1)}, bf16[128,12,128]{2,0,1:T(8,128)(2,1)}, u32[]{:S(2)}) copy-start(bf16[128,12,128]{2,0,1:T(8,128)(2,1)} %copy.98) | copy-start | bytes 1179652
  67.4 2.5 %copy-start.21 = (f32[12,128,352]{1,2,0:T(8,128)S(1)}, f32[12,128,352]{1,2,0:T(8,128)}, u32[]{:S(2)}) copy-start(f32[12,128,352]{1,2,0:T(8,128)} %copy-done.20) | copy-start | bytes 6488068
  67.4 2.5 %copy-start.22 = (bf16[128,12,128]{0,2,1:T(8,128)(2,1)S(1)}, bf16[128,12,128]{0,2,1:T(8,128)(2,1)}, u32[]{:S(2)}) copy-start(bf16[128,12,128]{0,2,1:T(8,128)(2,1)} %get-tuple-element.14) | copy-start | bytes 1179652
  69.7 1.8 copy-start.10
  74.2 1.3 copy-start
  79.2 9.6 %collective-permute-start.12 = (f32[2,32,1536]{2,1,0:T(8,128)S(1)}, f32[2,32,1536]{2,1,0:T(8,128)S(1)}, u32[]{:S(2)}, u32[]{:S(2)}) collective-permute-start(f32[2,32,1536]{2,1,0:T(8,128)S(1)} %fusion.35), channel_id=1, source_target_pairs={{0,4},{4,8},{8,12},{12,16},{16,20},{20,24},{24,28},{1,5},{5,9},{9,... | collective-permute-start | bytes 1179656 | tf_op jit(solution)/shard_map/ppermute | solution.py:13
  88.9 6.6 %collective-permute-start.13 = (f32[2,32,1536]{2,1,0:T(8,128)S(1)}, f32[2,32,1536]{2,1,0:T(8,128)S(1)}, u32[]{:S(2)}, u32[]{:S(2)}) collective-permute-start(f32[2,32,1536]{2,1,0:T(8,128)S(1)} %fusion.37), channel_id=1, source_target_pairs={{0,4},{4,8},{8,12},{12,16},{16,20},{20,24},{24,28},{1,5},{5,9},{9,... | collective-permute-start | bytes 1179656 | tf_op jit(solution)/shard_map/ppermute | solution.py:13
  96.3 9.0 %collective-permute-start.15 = (f32[2,32,1536]{2,1,0:T(8,128)S(1)}, f32[2,32,1536]{2,1,0:T(8,128)S(1)}, u32[]{:S(2)}, u32[]{:S(2)}) collective-permute-start(f32[2,32,1536]{2,1,0:T(8,128)S(1)} %get-tuple-element.16), channel_id=1, source_target_pairs={{4,0},{8,4},{12,8},{16,12},{20,16},{24,20},{28,24},{5,1},{9,5},{13... | collective-permute-start | bytes 1179656 | tf_op jit(solution)/shard_map/ppermute | solution.py:13
  106.1 20.5 %collective-permute-start.16 = (f32[2,32,1536]{2,1,0:T(8,128)}, f32[2,32,1536]{2,1,0:T(8,128)}, u32[]{:S(2)}, u32[]{:S(2)}) collective-permute-start(f32[2,32,1536]{2,1,0:T(8,128)} %fusion.30), channel_id=1, source_target_pairs={{4,0},{8,4},{12,8},{16,12},{20,16},{24,20},{28,24},{5,1},{9,5},{13... | collective-permute-start | bytes 1179656 | tf_op jit(solution)/shard_map/ppermute | solution.py:13
  109.3 5.9 %copy-start.2 = (bf16[224,12,128]{2,0,1:T(8,128)(2,1)S(1)}, bf16[224,12,128]{2,0,1:T(8,128)(2,1)}, u32[]{:S(2)}) copy-start(bf16[224,12,128]{2,0,1:T(8,128)(2,1)} %copy-done.1) | copy-start | bytes 2064388
  117.1 12.5 %copy-start.8 = (bf16[128,12,128]{0,2,1:T(8,128)(2,1)S(1)}, bf16[128,12,128]{0,2,1:T(8,128)(2,1)}, u32[]{:S(2)}) copy-start(bf16[128,12,128]{0,2,1:T(8,128)(2,1)} %copy.115) | copy-start | bytes 1179652
  117.1 12.5 %copy-start.9 = (bf16[128,12,128]{0,2,1:T(8,128)(2,1)S(1)}, bf16[128,12,128]{0,2,1:T(8,128)(2,1)}, u32[]{:S(2)}) copy-start(bf16[128,12,128]{0,2,1:T(8,128)(2,1)} %copy.113) | copy-start | bytes 1179652
  117.1 62.8 %collective-permute-start.14 = (f32[2,32,1536]{2,1,0:T(8,128)}, f32[2,32,1536]{2,1,0:T(8,128)S(1)}, u32[]{:S(2)}, u32[]{:S(2)}) collective-permute-start(f32[2,32,1536]{2,1,0:T(8,128)} %get-tuple-element.15), channel_id=1, source_target_pairs={{0,4},{4,8},{8,12},{12,16},{16,20},{20,24},{24,28},{1,5},{5,9},{9,... | collective-permute-start | bytes 1179656 | tf_op jit(solution)/shard_map/ppermute | solution.py:13
  128.3 51.6 %collective-permute-start.17 = (f32[2,32,1536]{2,1,0:T(8,128)}, f32[2,32,1536]{2,1,0:T(8,128)S(1)}, u32[]{:S(2)}, u32[]{:S(2)}) collective-permute-start(f32[2,32,1536]{2,1,0:T(8,128)} %fusion.41), channel_id=1, source_target_pairs={{4,0},{8,4},{12,8},{16,12},{20,16},{24,20},{28,24},{5,1},{9,5},{13... | collective-permute-start | bytes 1179656 | tf_op jit(solution)/shard_map/ppermute | solution.py:13
where the time goes:
time: 182 us; the launch traced here: 181 us
  starting transfers between devices  60.1 us (33%)
  blocking collectives  46.7 us (26%)
  local copies, waits for them, and re-layouts  32.3 us (18%)
  matrix products  18.1 us (10%)
  waiting for transfers between devices  10.8 us (6%)
  other arithmetic  8.28 us (5%)
  between operations  4.58 us (3%)
    ppermute x18, starting transfers between devices, from_behind(): return lax.ppermute(x, axis, pairs)  60.1 us
    psum x1, blocking collectives, body(): gamma_grad = lax.psum(contribution, ('seq', 'dp'))  46.7 us
    ppermute x18, waiting for transfers between devices, from_behind(): return lax.ppermute(x, axis, pairs)  10.8 us
    unnamed x64, local copies, waits for them, and re-layouts  9.62 us
    slice x2, local copies, waits for them, and re-layouts, body(): key_grad[:VB]  3.93 us
    slice x2, local copies, waits for them, and re-layouts, body(): value_grad[:VB]  3.88 us
    dot_general x1, matrix products, body(): jnp.einsum('hqk,khe->qhe', cond_probs, teach_values, preferred_element_ty...  3.68 us
  transfers between devices with their start and end apart: 18, of which 4 were waited for; matrix products, arithmetic and copies ran while one was open for 16% of the time, Pallas kernels for 0%

commit v1 on v0

v1 whole, which is shorter than its diff:
```python
import functools

import jax
import jax.numpy as jnp
from jax import lax
from jax.experimental import pallas as pl
from jax.experimental.pallas import tpu as pltpu
from jax.sharding import PartitionSpec as P

VB = 128
REACH = 3
SLOTS = 2 * REACH + 1
GROUPS = 4
MESH = pl.DeviceIdType.MESH
F32 = jnp.float32
BF16 = jnp.bfloat16


def dot(a, b, dims):
    return lax.dot_general(a, b, (dims, ((), ())), preferred_element_type=F32)


NT = ((1,), (1,))
NN = ((1,), (0,))
TN = ((0,), (0,))


def kernel(
    n, m, groups, heads,
    tv, sv, ta, sa, align, level_ref, step_ref, null_ref, gamma,
    gv_out, ga_out, gg_out,
    kv, qt, qs, gv, ga, pb, rp, rr, rd, ru, sdir, sind, suni, tot, gbuf, gbuf2, gout,
    load_sem, out_sem, in_send, in_recv, a_send, a_recv, g_send, g_recv, gam_send, gam_recv,
):
    width = tv.shape[-1]
    ta_len = ta.shape[2]
    hd = width // heads
    hpg = heads // groups
    gw = hpg * hd
    window = SLOTS * ta_len
    keys = VB + window
    scale = hd ** (-0.5)
    pairs = n // 2

    i = lax.axis_index("seq")
    z = lax.axis_index("dp")
    c = i % 2
    p = i // 2
    po = p % 2
    pe = 1 - po
    dirn = 1 - 2 * po
    d = 2 * c - 1
    partner = i - d
    lo_ok = i >= 2
    hi_ok = i + 2 < n
    ut = i + 3 * d
    u_ok = (ut >= 0) & (ut < n)
    u_slot = 6 * c
    relay = ((po == 0) & (p + 2 < pairs)) | ((po == 1) & (p >= 3))
    relay_direct = c == po
    relay_dev = i + 5 * pe - 1 - 3 * c
    ind_dev = i - 1 - 3 * pe + 5 * c
    ind_ok = ((po == 0) & lo_ok) | ((po == 1) & hi_ok)
    aff_dir = relay & relay_direct
    aff_uni = relay & jnp.logical_not(relay_direct)

    def krows(r):
        return pl.ds(pl.multiple_of(VB + ta_len * r, ta_len), ta_len)

    def prows(r):
        return pl.ds(pl.multiple_of(ta_len * r, ta_len), ta_len)

    def cols(g):
        return pl.ds(g * gw, gw)

    loads = [
        pltpu.make_async_copy(ta.at[0], kv.at[0:2, krows(REACH), :], load_sem.at[0]),
        pltpu.make_async_copy(sa.at[0], kv.at[2:4, krows(REACH), :], load_sem.at[1]),
        pltpu.make_async_copy(tv.at[0, 0], qt, load_sem.at[2]),
        pltpu.make_async_copy(tv.at[0, 1:3], kv.at[0:2, 0:VB, :], load_sem.at[3]),
        pltpu.make_async_copy(sv.at[0, 0], qs, load_sem.at[4]),
        pltpu.make_async_copy(sv.at[0, 1:3], kv.at[2:4, 0:VB, :], load_sem.at[5]),
    ]
    for load in loads:
        load.start()

    barrier = pltpu.get_barrier_semaphore()

    def greet_seq(k, carry):
        pl.semaphore_signal(barrier, inc=1, device_id={"seq": (i + k) % n}, device_id_type=MESH)
        return carry

    def greet_dp(k, carry):
        pl.semaphore_signal(barrier, inc=1, device_id={"dp": (z + k) % m}, device_id_type=MESH)
        return carry

    lax.fori_loop(1, n, greet_seq, 0)
    lax.fori_loop(1, m, greet_dp, 0)

    def clear(r):
        kv[:, krows(r), :] = jnp.zeros((4, ta_len, width), BF16)

    @pl.when(jnp.logical_not(lo_ok))
    def _():
        clear(1)
        clear(1 - d)

    @pl.when(jnp.logical_not(hi_ok))
    def _():
        clear(5)
        clear(5 - d)

    @pl.when(jnp.logical_not(u_ok))
    def _():
        clear(u_slot)
        ru[...] = jnp.zeros(ru.shape, BF16)

    tot[...] = jnp.zeros(tot.shape, F32)
    pl.semaphore_wait(barrier, (n - 1) + (m - 1))
    loads[0].wait()
    loads[1].wait()

    def in_copy(g, kind, src, dst, dev):
        return pltpu.make_async_remote_copy(
            src_ref=kv.at[:, krows(src), cols(g)],
            dst_ref=kv.at[:, krows(dst), cols(g)],
            send_sem=in_send.at[g, kind],
            recv_sem=in_recv.at[g, dst],
            device_id={"seq": dev},
            device_id_type=MESH,
        )

    def in_wait(g, r):
        ref = kv.at[:, krows(r), cols(g)]
        pltpu.make_async_copy(ref, ref, in_recv.at[g, r]).wait()

    relay_slot = jnp.where(relay_direct, 3 + 2 * dirn, u_slot)

    def in_sends(g):
        return (
            (in_copy(g, 0, REACH, 3 - 2 * dirn, i + 2 * dirn), None),
            (in_copy(g, 1, REACH, 3 - 3 * d, ut), u_ok),
            (in_copy(g, 2, REACH, 3 + d, partner), None),
            (in_copy(g, 3, relay_slot, 1 + 4 * c, relay_dev), relay),
            (in_copy(g, 4, 1, 1 + d, partner), lo_ok),
            (in_copy(g, 5, 5, 5 + d, partner), hi_ok),
        )

    def guarded(cond, act):
        if cond is None:
            act()
        else:
            pl.when(cond)(act)

    def own(g):
        for copy, cond in in_sends(g)[:3]:
            guarded(cond, copy.start)

    def forward(g):
        guarded(lo_ok, lambda: in_wait(g, 1))
        guarded(hi_ok, lambda: in_wait(g, 5))
        guarded(u_ok, lambda: in_wait(g, u_slot))
        for copy, cond in in_sends(g)[3:]:
            guarded(cond, copy.start)

    level = level_ref[0]
    weight = 1.0 + 0.75 * level.astype(F32)
    loss_weight = 1.0 / (1.0 + jnp.full((1, hd), step_ref[0], jnp.int32).astype(F32) / 250.0)
    first = align[0, 0, 0]
    count = align[0, 0, 1]
    keep = null_ref[0]
    kcol = lax.broadcasted_iota(jnp.int32, (VB, keys), 1)
    owner = i - REACH + (kcol - VB) // ta_len
    usable = (kcol < VB) | ((owner >= first) & (owner < first + count) & (keep == 0))

    def softmax(s):
        e = jnp.exp(s - jnp.max(s, axis=-1, keepdims=True))
        return e * (1.0 / jnp.sum(e, axis=-1, keepdims=True))

    def head(h):
        hc = pl.ds(h * hd, hd)
        k = kv[0, :, hc]
        v = kv[1, :, hc]
        s = dot(qt[:, hc], k, NT) * scale
        cond = dot(softmax(jnp.where(usable, s, -jnp.inf)).astype(BF16), v, NN)
        unc = dot(softmax(s[:, :VB]).astype(BF16), v[:VB], NN)
        target = unc + weight * (cond - unc)
        k = kv[2, :, hc]
        v = kv[3, :, hc]
        q = qs[:, hc]
        s = dot(q, k, NT) * scale
        probs = softmax(jnp.where(usable, s, -jnp.inf))
        pround = probs.astype(BF16)
        out = dot(pround, v, NN)
        factor = gamma[level, h]
        residual = loss_weight * (out * factor - target)
        tot[h : h + 1, :] = jnp.sum(residual * out, axis=0, keepdims=True)
        og = (residual * factor).astype(BF16)
        pg = dot(og, v, NT)
        delta = jnp.sum(og.astype(F32) * out, axis=-1, keepdims=True)
        sg = (scale * probs * (pg - delta)).astype(BF16)
        gv[0, :, hc] = dot(sg, k, NN).astype(BF16)
        kg = dot(sg, q, TN).astype(BF16)
        vg = dot(pround, og, TN).astype(BF16)
        gv[1, :, hc] = kg[:VB]
        gv[2, :, hc] = vg[:VB]
        pb[0, :, hc] = kg[VB:]
        pb[1, :, hc] = vg[VB:]

    def gv_copy(g):
        return pltpu.make_async_copy(gv.at[:, :, cols(g)], gv_out.at[0, :, :, cols(g)], out_sem.at[g])

    def compute(g):
        in_wait(g, 3 - d)
        guarded(lo_ok, lambda: in_wait(g, 1 - d))
        guarded(hi_ok, lambda: in_wait(g, 5 - d))
        if g == 0:
            for load in loads[2:]:
                load.wait()
        for h in range(g * hpg, (g + 1) * hpg):
            head(h)
        gv_copy(g).start()

    base = 1 - d

    def a_copies(g):
        return [
            pltpu.make_async_remote_copy(
                src_ref=pb.at[:, prows(base + 2 * k), cols(g)],
                dst_ref=rp.at[k, :, :, cols(g)],
                send_sem=a_send.at[g, k],
                recv_sem=a_recv.at[g, k],
                device_id={"seq": partner},
                device_id_type=MESH,
            )
            for k in range(3)
        ]

    def stage_a(g):
        for copy in a_copies(g):
            copy.start()

    def g_copy(g, kind, src, dst, dev):
        return pltpu.make_async_remote_copy(
            src_ref=src,
            dst_ref=dst.at[:, :, cols(g)],
            send_sem=g_send.at[g, kind],
            recv_sem=g_recv.at[g, kind],
            device_id={"seq": dev},
            device_id_type=MESH,
        )

    def dir_copy(g):
        return g_copy(g, 0, sdir.at[:, :, cols(g)], rd, i + 2 * dirn)

    def uni_copy(g):
        return g_copy(g, 1, suni.at[:, :, cols(g)], ru, ut)

    def uni_plain(g):
        return g_copy(g, 1, pb.at[:, prows(u_slot), cols(g)], ru, ut)

    def ind_copy(g):
        return g_copy(g, 2, sind.at[:, :, cols(g)], rr, ind_dev)

    def stage_b(g):
        for copy in a_copies(g):
            copy.wait_recv()
        cs = cols(g)

        @pl.when(ind_ok)
        def _():
            sind[:, :, cs] = (
                pb[:, prows(3 - 2 * dirn), cs].astype(F32) + rp[1 - dirn, :, :, cs].astype(F32)
            ).astype(BF16)
            ind_copy(g).start()

        pl.when(u_ok & jnp.logical_not(aff_uni))(uni_plain(g).start)

        @pl.when(jnp.logical_not(aff_dir))
        def _():
            sdir[:, :, cs] = (
                pb[:, prows(3 + 2 * dirn), cs].astype(F32) + rp[1 + dirn, :, :, cs].astype(F32)
            ).astype(BF16)
            dir_copy(g).start()

    def stage_c(g):
        cs = cols(g)
        pl.when(relay)(lambda: ind_copy(g).wait_recv())

        @pl.when(aff_dir)
        def _():
            sdir[:, :, cs] = (
                pb[:, prows(3 + 2 * dirn), cs].astype(F32)
                + rp[1 + dirn, :, :, cs].astype(F32)
                + rr[:, :, cs].astype(F32)
            ).astype(BF16)
            dir_copy(g).start()

        @pl.when(aff_uni)
        def _():
            suni[:, :, cs] = (
                pb[:, prows(u_slot), cs].astype(F32) + rr[:, :, cs].astype(F32)
            ).astype(BF16)
            uni_copy(g).start()

    def stage_d(g):
        cs = cols(g)
        dir_copy(g).wait_recv()
        pl.when(u_ok)(lambda: uni_copy(g).wait_recv())
        ga[:, :, cs] = (
            pb[:, prows(REACH), cs].astype(F32)
            + rp[1, :, :, cs].astype(F32)
            + rd[:, :, cs].astype(F32)
            + ru[:, :, cs].astype(F32)
        ).astype(BF16)

    def gam_exchange(buf, which, size, me, axis):
        def send(k, carry):
            pltpu.make_async_remote_copy(
                src_ref=buf.at[me],
                dst_ref=buf.at[me],
                send_sem=gam_send.at[which],
                recv_sem=gam_recv.at[which],
                device_id={axis: (me + k) % size},
                device_id_type=MESH,
            ).start()
            return carry

        lax.fori_loop(1, size, send, 0)

    def gam_wait(buf, which, size, sem):
        ref = buf.at[0 : size - 1]
        pltpu.make_async_copy(ref, ref, sem.at[which]).wait()

    def gamma_first():
        sums = jnp.sum(tot[...], axis=-1, keepdims=True)
        rows = lax.broadcasted_iota(jnp.int32, tot.shape, 0)
        lanes = lax.broadcasted_iota(jnp.int32, tot.shape, 1)
        vec = jnp.sum(jnp.where(rows == lanes, sums, 0.0), axis=0, keepdims=True)
        vec = vec / (VB * n * hd)
        levels = lax.broadcasted_iota(jnp.int32, gbuf.shape[1:], 0)
        gbuf[i] = jnp.where(levels == level, vec, 0.0)
        gam_exchange(gbuf, 0, n, i, "seq")

    def gamma_second():
        gam_wait(gbuf, 0, n, gam_recv)
        gbuf2[z] = jnp.sum(gbuf[...], axis=0)
        gam_exchange(gbuf2, 1, m, z, "dp")

    def gamma_last():
        gam_wait(gbuf2, 1, m, gam_recv)
        gout[...] = jnp.sum(gbuf2[...], axis=0)[:, : gout.shape[1]]

    own(0)
    for t in range(groups + 4):
        if t + 1 < groups:
            own(t + 1)
        if t < groups:
            forward(t)
        if 0 <= t - 1 < groups:
            compute(t - 1)
            stage_a(t - 1)
            if t - 1 == groups - 1:
                gamma_first()
        if 0 <= t - 2 < groups:
            stage_b(t - 2)
        if 0 <= t - 3 < groups:
            stage_c(t - 3)
        if t == groups + 2:
            gamma_second()
        if 0 <= t - 4 < groups:
            stage_d(t - 4)
    ga_copy = pltpu.make_async_copy(ga, ga_out.at[0], load_sem.at[0])
    ga_copy.start()
    gamma_last()
    gg_copy = pltpu.make_async_copy(gout, gg_out, load_sem.at[1])
    gg_copy.start()
    for g in range(groups):
        gv_copy(g).wait()
        for copy, cond in in_sends(g):
            guarded(cond, copy.wait_send)
        for copy in a_copies(g):
            copy.wait_send()
        dir_copy(g).wait_send()
        pl.when(u_ok)(lambda: uni_copy(g).wait_send())
        pl.when(ind_ok)(lambda: ind_copy(g).wait_send())
    gam_wait(gbuf, 0, n, gam_send)
    gam_wait(gbuf2, 1, m, gam_send)
    ga_copy.wait()
    gg_copy.wait()


def body(n, m, tv, sv, ta, sa, align, level, step, null, gamma):
    width = tv.shape[-1]
    ta_len = ta.shape[2]
    glevels, heads = gamma.shape
    groups = GROUPS
    window = SLOTS * ta_len
    keys = VB + window
    any_spec = pl.BlockSpec(memory_space=pl.ANY)
    smem = pl.BlockSpec(memory_space=pltpu.SMEM)
    piece = pltpu.VMEM((2, ta_len, width), BF16)
    dma = pltpu.SemaphoreType.DMA
    return pl.pallas_call(
        functools.partial(kernel, n, m, groups, heads),
        out_shape=(
            jax.ShapeDtypeStruct(tv.shape, BF16),
            jax.ShapeDtypeStruct(ta.shape, BF16),
            jax.ShapeDtypeStruct(gamma.shape, F32),
        ),
        in_specs=[any_spec] * 4 + [smem] * 5,
        out_specs=(any_spec, any_spec, any_spec),
        scratch_shapes=[
            pltpu.VMEM((4, keys, width), BF16),
            pltpu.VMEM((VB, width), BF16),
            pltpu.VMEM((VB, width), BF16),
            pltpu.VMEM((3, VB, width), BF16),
            piece,
            pltpu.VMEM((2, window, width), BF16),
            pltpu.VMEM((3, 2, ta_len, width), BF16),
            piece, piece, piece, piece, piece, piece,
            pltpu.VMEM((-(-heads // 8) * 8, 128), F32),
            pltpu.VMEM((n, glevels, 128), F32),
            pltpu.VMEM((m, glevels, 128), F32),
            pltpu.VMEM((glevels, heads), F32),
            dma((6,)),
            dma((groups,)),
            dma((groups, 6)),
            dma((groups, SLOTS)),
            dma((groups, 3)),
            dma((groups, 3)),
            dma((groups, 3)),
            dma((groups, 3)),
            dma((2,)),
            dma((2,)),
        ],
        compiler_params=pltpu.CompilerParams(
            collective_id=0, has_side_effects=True, vmem_limit_bytes=48 * 1024 * 1024
        ),
    )(tv, sv, ta, sa, align, level, step, null, gamma)


def solution(mesh):
    return jax.shard_map(
        functools.partial(body, mesh.shape["seq"], mesh.shape["dp"]),
        mesh=mesh,
        in_specs=(
            P("dp", None, "seq", None),
            P("dp", None, "seq", None),
            P("dp", None, "seq", None),
            P("dp", None, "seq", None),
            P("dp", "seq", None),
            P("dp"),
            P("dp"),
            P("dp"),
            P(),
        ),
        out_specs=(P("dp", None, "seq", None), P("dp", None, "seq", None), P()),
        check_vma=False,
    )
```

time: 182 us -> 54.5 us (0.30)
  starting transfers between devices: 60.1 us -> 0 us
  blocking collectives: 46.7 us -> 0 us
  Pallas kernels: 0 us -> 43.6 us
  local copies, waits for them, and re-layouts: 32.3 us -> 8.01 us
  matrix products: 18.1 us -> 0 us
  waiting for transfers between devices: 10.8 us -> 0 us
  other arithmetic: 8.28 us -> 0 us
  between operations: 4.58 us -> 2.59 us
    ppermute x18 -> x0, starting transfers between devices: 60.1 us -> none  [from_behind(): return lax.ppermute(x, axis, pairs)]
    psum x1 -> x0, blocking collectives: 46.7 us -> none  [body(): gamma_grad = lax.psum(contribution, ('seq', 'dp'))]
    pallas_call x0 -> x1, Pallas kernels: none -> 43.6 us  [body(): pl.pallas_call(functools.partial(kernel, n, m, groups, heads), out_shape=...]
    dot_general x9 -> x0, matrix products: 17.3 us -> none  [the longest x1 3.68 us: body(): jnp.einsum('hqk,khe->qhe', cond_probs, teach_values, preferred_element_ty...]
    slice x18 -> x0, local copies, waits for them, and re-layouts: 13.6 us -> none  [the longest x2 3.93 us: body(): key_grad[:VB]]
    ppermute x18 -> x0, waiting for transfers between devices: 10.8 us -> none  [from_behind(): return lax.ppermute(x, axis, pairs)]
    squeeze x8 -> x0, local copies, waits for them, and re-layouts: 6.7 us -> none  [the longest x2 2.06 us: body(): pupil_values = jnp.concatenate([pupil_vid[2, 0], pupil_window[1]], axis=0)]
    add x4 -> x0, other arithmetic: 3.5 us -> none  [the longest x2 2.62 us: body(): gathered_low = from_behind(gathered_low + slot_piece(offset), 'seq', -1)]
  transfers between devices with their start and end apart: 18 -> 0, of which waited for: 4 -> 0; matrix products, arithmetic and copies ran while one was open for 16% -> 0% of each run, Pallas kernels for 0% -> 0%
where the time goes in v1:
time: 54.5 us; the launch traced here: 54.2 us
  Pallas kernels  43.6 us (80%)
  local copies, waits for them, and re-layouts  8.01 us (15%)
  between operations  2.59 us (5%)
    pallas_call x1, Pallas kernels, body(): pl.pallas_call(functools.partial(kernel, n, m, groups, heads), out_shape=...  43.6 us
    unnamed x15, local copies, waits for them, and re-layouts  8.01 us

profile of v1, /device:TPU:0, one launch (start us, length us, event | category | flops | bytes accessed | tf_op | source)
XLA Modules:
  0.0 54.2 jit_solution(7780181322059792811)
XLA Ops:
  2.6 0.0 copy-start
  2.6 1.3 %copy-done = bf16[1,3,128,1536]{3,2,1,0:T(8,128)(2,1)S(1)} copy-done((bf16[1,3,128,1536]{3,2,1,0:T(8,128)(2,1)S(1)}, bf16[1,3,128,1536]{3,2,1,0:T(8,128)(2,1)}, u32[]{:S(2)}) %copy-start) | copy-done | bytes 1179672
  3.8 0.0 copy-start.1
  3.8 1.3 %copy-done.1 = bf16[1,3,128,1536]{3,2,1,0:T(8,128)(2,1)S(1)} copy-done((bf16[1,3,128,1536]{3,2,1,0:T(8,128)(2,1)S(1)}, bf16[1,3,128,1536]{3,2,1,0:T(8,128)(2,1)}, u32[]{:S(2)}) %copy-start.1) | copy-done | bytes 1179672
  5.1 0.0 copy-start.2
  5.1 0.9 %copy-done.2 = bf16[1,2,32,1536]{3,2,1,0:T(8,128)(2,1)S(1)} copy-done((bf16[1,2,32,1536]{3,2,1,0:T(8,128)(2,1)S(1)}, bf16[1,2,32,1536]{3,2,1,0:T(8,128)(2,1)}, u32[]{:S(2)}) %copy-start.2) | copy-done | bytes 196632
  6.0 0.0 copy-start.3
  6.0 0.9 %copy-done.3 = bf16[1,2,32,1536]{3,2,1,0:T(8,128)(2,1)S(1)} copy-done((bf16[1,2,32,1536]{3,2,1,0:T(8,128)(2,1)S(1)}, bf16[1,2,32,1536]{3,2,1,0:T(8,128)(2,1)}, u32[]{:S(2)}) %copy-start.3) | copy-done | bytes 196632
  7.0 0.0 copy-start.4
  7.0 0.7 %copy-done.4 = f32[8,12]{1,0:T(8,128)S(1)} copy-done((f32[8,12]{1,0:T(8,128)S(1)}, f32[8,12]{1,0:T(8,128)}, u32[]{:S(2)}) %copy-start.4) | copy-done | bytes 408
  7.7 0.0 copy-start.5
  7.7 0.7 %copy-done.5 = s32[1,1,2]{2,1,0:T(1,128)S(1)} copy-done((s32[1,1,2]{2,1,0:T(1,128)S(1)}, s32[1,1,2]{2,1,0:T(1,128)}, u32[]{:S(2)}) %copy-start.5) | copy-done | bytes 32
  8.3 43.6 %shard_map.112 = (bf16[1,3,128,1536]{3,2,1,0:T(8,128)(2,1)S(1)}, bf16[1,2,32,1536]{3,2,1,0:T(8,128)(2,1)S(1)}, f32[8,12]{1,0:T(8,128)S(1)}) custom-call(bf16[1,3,128,1536]{3,2,1,0:T(8,128)(2,1)S(1)} %copy-done, bf16[1,3,128,1536]{3,2,1,0:T(8,128)(2,1)S(1)} %copy-done.1, bf16[1,2,32,1536]{3,2,1,0:T(8,128)(2,1)S(1)} %copy-done.2, ...), custom_call_target="tpu_custom_call" | custom-call | tf_op jit(solution)/shard_map/pallas_call | solution.py:404
  51.9 1.0 %copy.18 = bf16[1,3,128,1536]{3,2,1,0:T(8,128)(2,1)} copy(bf16[1,3,128,1536]{3,2,1,0:T(8,128)(2,1)S(1)} %get-tuple-element.6) | data formatting | bytes 2359296
  52.9 0.7 %copy.19 = bf16[1,2,32,1536]{3,2,1,0:T(8,128)(2,1)} copy(bf16[1,2,32,1536]{3,2,1,0:T(8,128)(2,1)S(1)} %get-tuple-element.7) | data formatting | bytes 393216
  53.6 0.6 %copy.20 = f32[8,12]{1,0:T(8,128)} copy(f32[8,12]{1,0:T(8,128)S(1)} %get-tuple-element.8) | data formatting | bytes 768
Async XLA Ops:
  2.6 1.3 %copy-start = (bf16[1,3,128,1536]{3,2,1,0:T(8,128)(2,1)S(1)}, bf16[1,3,128,1536]{3,2,1,0:T(8,128)(2,1)}, u32[]{:S(2)}) copy-start(bf16[1,3,128,1536]{3,2,1,0:T(8,128)(2,1)} %tv.1) | copy-start | bytes 3538948
  3.8 1.3 %copy-start.1 = (bf16[1,3,128,1536]{3,2,1,0:T(8,128)(2,1)S(1)}, bf16[1,3,128,1536]{3,2,1,0:T(8,128)(2,1)}, u32[]{:S(2)}) copy-start(bf16[1,3,128,1536]{3,2,1,0:T(8,128)(2,1)} %sv.1) | copy-start | bytes 3538948
  5.1 0.9 %copy-start.2 = (bf16[1,2,32,1536]{3,2,1,0:T(8,128)(2,1)S(1)}, bf16[1,2,32,1536]{3,2,1,0:T(8,128)(2,1)}, u32[]{:S(2)}) copy-start(bf16[1,2,32,1536]{3,2,1,0:T(8,128)(2,1)} %ta.1) | copy-start | bytes 589828
  6.0 0.9 %copy-start.3 = (bf16[1,2,32,1536]{3,2,1,0:T(8,128)(2,1)S(1)}, bf16[1,2,32,1536]{3,2,1,0:T(8,128)(2,1)}, u32[]{:S(2)}) copy-start(bf16[1,2,32,1536]{3,2,1,0:T(8,128)(2,1)} %sa.1) | copy-start | bytes 589828
  7.0 0.7 %copy-start.4 = (f32[8,12]{1,0:T(8,128)S(1)}, f32[8,12]{1,0:T(8,128)}, u32[]{:S(2)}) copy-start(f32[8,12]{1,0:T(8,128)} %gamma.1) | copy-start | bytes 1156
  7.7 0.7 %copy-start.5 = (s32[1,1,2]{2,1,0:T(1,128)S(1)}, s32[1,1,2]{2,1,0:T(1,128)}, u32[]{:S(2)}) copy-start(s32[1,1,2]{2,1,0:T(1,128)} %align.1) | copy-start | bytes 28

commit v2 on v1

--- a/solution.py
+++ b/solution.py
@@ -27,9 +27,10 @@
 
 def kernel(
     n, m, groups, heads,
-    tv, sv, ta, sa, align, level_ref, step_ref, null_ref, gamma,
+    tv, sv, ta, sa, align_in, level_in, step_in, null_in, gamma_in,
     gv_out, ga_out, gg_out,
-    kv, qt, qs, gv, ga, pb, rp, rr, rd, ru, sdir, sind, suni, tot, gbuf, gbuf2, gout,
+    kv, qt, qs, gv, ga, pb, rp, rr, rd, ru, sdir, sind, suni, tot, gbuf, gbuf2, gout, un, st, ss,
+    align, level_ref, step_ref, null_ref, gamma,
     load_sem, out_sem, in_send, in_recv, a_send, a_recv, g_send, g_recv, gam_send, gam_recv,
 ):
     width = tv.shape[-1]
@@ -57,12 +58,21 @@
     u_ok = (ut >= 0) & (ut < n)
     u_slot = 6 * c
     relay = ((po == 0) & (p + 2 < pairs)) | ((po == 1) & (p >= 3))
-    relay_direct = c == po
-    relay_dev = i + 5 * pe - 1 - 3 * c
-    ind_dev = i - 1 - 3 * pe + 5 * c
+    first_way = c == po
     ind_ok = ((po == 0) & lo_ok) | ((po == 1) & hi_ok)
-    aff_dir = relay & relay_direct
-    aff_uni = relay & jnp.logical_not(relay_direct)
+
+    def way(g):
+        direct_slot = 3 + 2 * dirn
+        if g % 2 == 1:
+            return direct_slot, 3 - 2 * dirn, i + 4 * dirn, i - 4 * dirn, relay, None
+        return (
+            jnp.where(first_way, direct_slot, u_slot),
+            1 + 4 * c,
+            i + 5 * pe - 1 - 3 * c,
+            i - 1 - 3 * pe + 5 * c,
+            relay & first_way,
+            relay & jnp.logical_not(first_way),
+        )
 
     def krows(r):
         return pl.ds(pl.multiple_of(VB + ta_len * r, ta_len), ta_len)
@@ -80,6 +90,11 @@
         pltpu.make_async_copy(tv.at[0, 1:3], kv.at[0:2, 0:VB, :], load_sem.at[3]),
         pltpu.make_async_copy(sv.at[0, 0], qs, load_sem.at[4]),
         pltpu.make_async_copy(sv.at[0, 1:3], kv.at[2:4, 0:VB, :], load_sem.at[5]),
+        pltpu.make_async_copy(align_in, align, load_sem.at[6]),
+        pltpu.make_async_copy(level_in, level_ref, load_sem.at[7]),
+        pltpu.make_async_copy(step_in, step_ref, load_sem.at[8]),
+        pltpu.make_async_copy(null_in, null_ref, load_sem.at[9]),
+        pltpu.make_async_copy(gamma_in, gamma, load_sem.at[10]),
     ]
     for load in loads:
         load.start()
@@ -119,6 +134,8 @@
     pl.semaphore_wait(barrier, (n - 1) + (m - 1))
     loads[0].wait()
     loads[1].wait()
+    for load in loads[6:]:
+        load.wait()
 
     def in_copy(g, kind, src, dst, dev):
         return pltpu.make_async_remote_copy(
@@ -134,14 +151,13 @@
         ref = kv.at[:, krows(r), cols(g)]
         pltpu.make_async_copy(ref, ref, in_recv.at[g, r]).wait()
 
-    relay_slot = jnp.where(relay_direct, 3 + 2 * dirn, u_slot)
-
     def in_sends(g):
+        relay_slot, relay_dst, relay_dev = way(g)[:3]
         return (
             (in_copy(g, 0, REACH, 3 - 2 * dirn, i + 2 * dirn), None),
             (in_copy(g, 1, REACH, 3 - 3 * d, ut), u_ok),
             (in_copy(g, 2, REACH, 3 + d, partner), None),
-            (in_copy(g, 3, relay_slot, 1 + 4 * c, relay_dev), relay),
+            (in_copy(g, 3, relay_slot, relay_dst, relay_dev), relay),
             (in_copy(g, 4, 1, 1 + d, partner), lo_ok),
             (in_copy(g, 5, 5, 5 + d, partner), hi_ok),
         )
@@ -177,18 +193,27 @@
         e = jnp.exp(s - jnp.max(s, axis=-1, keepdims=True))
         return e * (1.0 / jnp.sum(e, axis=-1, keepdims=True))
 
+    def head_local(h):
+        hc = pl.ds(h * hd, hd)
+        sc = pl.ds(h * VB, VB)
+        s = dot(qt[:, hc], kv[0, :VB, hc], NT) * scale
+        st[:, sc] = s
+        un[:, hc] = dot(softmax(s).astype(BF16), kv[1, :VB, hc], NN)
+        ss[:, sc] = dot(qs[:, hc], kv[2, :VB, hc], NT) * scale
+
     def head(h):
         hc = pl.ds(h * hd, hd)
-        k = kv[0, :, hc]
+        sc = pl.ds(h * VB, VB)
         v = kv[1, :, hc]
-        s = dot(qt[:, hc], k, NT) * scale
+        s = dot(qt[:, hc], kv[0, VB:, hc], NT) * scale
+        s = jnp.concatenate([st[:, sc], s], axis=1)
         cond = dot(softmax(jnp.where(usable, s, -jnp.inf)).astype(BF16), v, NN)
-        unc = dot(softmax(s[:, :VB]).astype(BF16), v[:VB], NN)
+        unc = un[:, hc]
         target = unc + weight * (cond - unc)
         k = kv[2, :, hc]
         v = kv[3, :, hc]
         q = qs[:, hc]
-        s = dot(q, k, NT) * scale
+        s = jnp.concatenate([ss[:, sc], dot(q, k[VB:], NT) * scale], axis=1)
         probs = softmax(jnp.where(usable, s, -jnp.inf))
         pround = probs.astype(BF16)
         out = dot(pround, v, NN)
@@ -214,9 +239,6 @@
         in_wait(g, 3 - d)
         guarded(lo_ok, lambda: in_wait(g, 1 - d))
         guarded(hi_ok, lambda: in_wait(g, 5 - d))
-        if g == 0:
-            for load in loads[2:]:
-                load.wait()
         for h in range(g * hpg, (g + 1) * hpg):
             head(h)
         gv_copy(g).start()
@@ -260,7 +282,7 @@
         return g_copy(g, 1, pb.at[:, prows(u_slot), cols(g)], ru, ut)
 
     def ind_copy(g):
-        return g_copy(g, 2, sind.at[:, :, cols(g)], rr, ind_dev)
+        return g_copy(g, 2, sind.at[:, :, cols(g)], rr, way(g)[3])
 
     def stage_b(g):
         for copy in a_copies(g):
@@ -274,7 +296,9 @@
             ).astype(BF16)
             ind_copy(g).start()
 
-        pl.when(u_ok & jnp.logical_not(aff_uni))(uni_plain(g).start)
+        aff_dir, aff_uni = way(g)[4:]
+        plain = u_ok if aff_uni is None else u_ok & jnp.logical_not(aff_uni)
+        pl.when(plain)(uni_plain(g).start)
 
         @pl.when(jnp.logical_not(aff_dir))
         def _():
@@ -285,6 +309,7 @@
 
     def stage_c(g):
         cs = cols(g)
+        aff_dir, aff_uni = way(g)[4:]
         pl.when(relay)(lambda: ind_copy(g).wait_recv())
 
         @pl.when(aff_dir)
@@ -295,6 +320,9 @@
                 + rr[:, :, cs].astype(F32)
             ).astype(BF16)
             dir_copy(g).start()
+
+        if aff_uni is None:
+            return
 
         @pl.when(aff_uni)
         def _():
@@ -352,9 +380,14 @@
         gout[...] = jnp.sum(gbuf2[...], axis=0)[:, : gout.shape[1]]
 
     own(0)
+    for load in loads[2:6]:
+        load.wait()
     for t in range(groups + 4):
         if t + 1 < groups:
             own(t + 1)
+        if t == 0:
+            for h in range(heads):
+                head_local(h)
         if t < groups:
             forward(t)
         if 0 <= t - 1 < groups:
@@ -364,10 +397,10 @@
                 gamma_first()
         if 0 <= t - 2 < groups:
             stage_b(t - 2)
+        if t == groups + 2:
+            gamma_second()
         if 0 <= t - 3 < groups:
             stage_c(t - 3)
-        if t == groups + 2:
-            gamma_second()
         if 0 <= t - 4 < groups:
             stage_d(t - 4)
     ga_copy = pltpu.make_async_copy(ga, ga_out.at[0], load_sem.at[0])
@@ -398,7 +431,7 @@
     window = SLOTS * ta_len
     keys = VB + window
     any_spec = pl.BlockSpec(memory_space=pl.ANY)
-    smem = pl.BlockSpec(memory_space=pltpu.SMEM)
+    hbm_spec = pl.BlockSpec(memory_space=pltpu.HBM)
     piece = pltpu.VMEM((2, ta_len, width), BF16)
     dma = pltpu.SemaphoreType.DMA
     return pl.pallas_call(
@@ -408,7 +441,7 @@
             jax.ShapeDtypeStruct(ta.shape, BF16),
             jax.ShapeDtypeStruct(gamma.shape, F32),
         ),
-        in_specs=[any_spec] * 4 + [smem] * 5,
+        in_specs=[hbm_spec] * 9,
         out_specs=(any_spec, any_spec, any_spec),
         scratch_shapes=[
             pltpu.VMEM((4, keys, width), BF16),
@@ -423,7 +456,15 @@
             pltpu.VMEM((n, glevels, 128), F32),
             pltpu.VMEM((m, glevels, 128), F32),
             pltpu.VMEM((glevels, heads), F32),
-            dma((6,)),
+            pltpu.VMEM((VB, width), F32),
+            pltpu.VMEM((VB, heads * VB), F32),
+            pltpu.VMEM((VB, heads * VB), F32),
+            pltpu.SMEM(align.shape, jnp.int32),
+            pltpu.SMEM(level.shape, jnp.int32),
+            pltpu.SMEM(step.shape, jnp.int32),
+            pltpu.SMEM(null.shape, jnp.int32),
+            pltpu.SMEM(gamma.shape, F32),
+            dma((11,)),
             dma((groups,)),
             dma((groups, 6)),
             dma((groups, SLOTS)),
@@ -435,7 +476,7 @@
             dma((2,)),
         ],
         compiler_params=pltpu.CompilerParams(
-            collective_id=0, has_side_effects=True, vmem_limit_bytes=48 * 1024 * 1024
+            collective_id=0, has_side_effects=True
         ),
     )(tv, sv, ta, sa, align, level, step, null, gamma)
 

time: 54.5 us -> 48 us (0.88)
  local copies, waits for them, and re-layouts: 8.01 us -> 3.68 us
  Pallas kernels: 43.6 us -> 41.6 us
    unnamed x15 -> x7, local copies, waits for them, and re-layouts: 8.01 us -> 3.68 us
    pallas_call x1, Pallas kernels: 43.6 us -> 41.6 us  [body(): pl.pallas_call(functools.partial(kernel, n, m, groups, heads), out_shape=...]
where the time goes in v2:
time: 48 us; the launch traced here: 47.9 us
  Pallas kernels  41.6 us (87%)
  local copies, waits for them, and re-layouts  3.68 us (8%)
  between operations  2.59 us (5%)
    pallas_call x1, Pallas kernels, body(): pl.pallas_call(functools.partial(kernel, n, m, groups, heads), out_shape=...  41.6 us
    unnamed x7, local copies, waits for them, and re-layouts  3.68 us

profile of v2, /device:TPU:0, one launch (start us, length us, event | category | flops | bytes accessed | tf_op | source)
XLA Modules:
  0.0 47.9 jit_solution(8908563833421800778)
XLA Ops:
  2.6 41.6 %shard_map.112 = (bf16[1,3,128,1536]{3,2,1,0:T(8,128)(2,1)}, bf16[1,2,32,1536]{3,2,1,0:T(8,128)(2,1)}, f32[8,12]{1,0:T(8,128)}) custom-call(bf16[1,3,128,1536]{3,2,1,0:T(8,128)(2,1)} %tv.1, bf16[1,3,128,1536]{3,2,1,0:T(8,128)(2,1)} %sv.1, bf16[1,2,32,1536]{3,2,1,0:T(8,128)(2,1)} %ta.1, bf16[1,2,32,1536]{3,2,1,0:T(8,128)(2,1)} %sa.1, s32[1,1,2]{2,1,0:T(1,128)} %align_in.1, ...), custom_call_target="tpu_custom_call" | custom-call | tf_op jit(solution)/shard_map/pallas_call | solution.py:437
  44.2 0.0 copy-start
  44.2 0.0 copy-start.1
  44.2 2.4 %copy.18 = bf16[1,3,128,1536]{3,2,1,0:T(8,128)(2,1)} copy(bf16[1,3,128,1536]{3,2,1,0:T(8,128)(2,1)} %get-tuple-element.6) | data formatting | bytes 2359296
  46.6 0.0 copy-done
  46.6 0.7 %copy.19 = bf16[1,2,32,1536]{3,2,1,0:T(8,128)(2,1)} copy(bf16[1,2,32,1536]{3,2,1,0:T(8,128)(2,1)S(1)} %copy-done) | data formatting | bytes 393216
  47.3 0.0 copy-done.1
  47.3 0.6 %copy.20 = f32[8,12]{1,0:T(8,128)} copy(f32[8,12]{1,0:T(8,128)S(1)} %copy-done.1) | data formatting | bytes 768
Async XLA Ops:
  44.2 2.4 %copy-start = (bf16[1,2,32,1536]{3,2,1,0:T(8,128)(2,1)S(1)}, bf16[1,2,32,1536]{3,2,1,0:T(8,128)(2,1)}, u32[]{:S(2)}) copy-start(bf16[1,2,32,1536]{3,2,1,0:T(8,128)(2,1)} %get-tuple-element.7) | copy-start | bytes 589828
  44.2 3.1 %copy-start.1 = (f32[8,12]{1,0:T(8,128)S(1)}, f32[8,12]{1,0:T(8,128)}, u32[]{:S(2)}) copy-start(f32[8,12]{1,0:T(8,128)} %get-tuple-element.8) | copy-start | bytes 1156

commit v3 on v2

--- a/solution.py
+++ b/solution.py
@@ -173,11 +173,28 @@
             guarded(cond, copy.start)
 
     def forward(g):
-        guarded(lo_ok, lambda: in_wait(g, 1))
-        guarded(hi_ok, lambda: in_wait(g, 5))
         guarded(u_ok, lambda: in_wait(g, u_slot))
-        for copy, cond in in_sends(g)[3:]:
-            guarded(cond, copy.start)
+        relayed, low, high = in_sends(g)[3:]
+
+        def pass_low():
+            in_wait(g, 1)
+            low[0].start()
+
+        def pass_high():
+            in_wait(g, 5)
+            high[0].start()
+
+        @pl.when(po == 0)
+        def _():
+            guarded(hi_ok, pass_high)
+            guarded(relayed[1], relayed[0].start)
+            guarded(lo_ok, pass_low)
+
+        @pl.when(po == 1)
+        def _():
+            guarded(lo_ok, pass_low)
+            guarded(relayed[1], relayed[0].start)
+            guarded(hi_ok, pass_high)
 
     level = level_ref[0]
     weight = 1.0 + 0.75 * level.astype(F32)
@@ -379,12 +396,11 @@
         gam_wait(gbuf2, 1, m, gam_recv)
         gout[...] = jnp.sum(gbuf2[...], axis=0)[:, : gout.shape[1]]
 
-    own(0)
+    for g in range(groups):
+        own(g)
     for load in loads[2:6]:
         load.wait()
     for t in range(groups + 4):
-        if t + 1 < groups:
-            own(t + 1)
         if t == 0:
             for h in range(heads):
                 head_local(h)

time: 48 us -> 45.6 us (0.950)
  Pallas kernels: 41.6 us -> 39.2 us
    pallas_call x1, Pallas kernels: 41.6 us -> 39.2 us  [body(): pl.pallas_call(functools.partial(kernel, n, m, groups, heads), out_shape=...]
where the time goes in v3:
time: 45.6 us; the launch traced here: 45.4 us
  Pallas kernels  39.2 us (86%)
  local copies, waits for them, and re-layouts  3.68 us (8%)
  between operations  2.59 us (6%)
    pallas_call x1, Pallas kernels, body(): pl.pallas_call(functools.partial(kernel, n, m, groups, heads), out_shape=...  39.2 us
    unnamed x7, local copies, waits for them, and re-layouts  3.68 us

profile of v3, /device:TPU:0, one launch (start us, length us, event | category | flops | bytes accessed | tf_op | source)
XLA Modules:
  0.0 45.4 jit_solution(4861823752417522096)
XLA Ops:
  2.6 39.2 %shard_map.112 = (bf16[1,3,128,1536]{3,2,1,0:T(8,128)(2,1)}, bf16[1,2,32,1536]{3,2,1,0:T(8,128)(2,1)}, f32[8,12]{1,0:T(8,128)}) custom-call(bf16[1,3,128,1536]{3,2,1,0:T(8,128)(2,1)} %tv.1, bf16[1,3,128,1536]{3,2,1,0:T(8,128)(2,1)} %sv.1, bf16[1,2,32,1536]{3,2,1,0:T(8,128)(2,1)} %ta.1, bf16[1,2,32,1536]{3,2,1,0:T(8,128)(2,1)} %sa.1, s32[1,1,2]{2,1,0:T(1,128)} %align_in.1, ...), custom_call_target="tpu_custom_call" | custom-call | tf_op jit(solution)/shard_map/pallas_call | solution.py:453
  41.8 0.0 copy-start
  41.8 0.0 copy-start.1
  41.8 2.4 %copy.18 = bf16[1,3,128,1536]{3,2,1,0:T(8,128)(2,1)} copy(bf16[1,3,128,1536]{3,2,1,0:T(8,128)(2,1)} %get-tuple-element.6) | data formatting | bytes 2359296
  44.2 0.0 copy-done
  44.2 0.7 %copy.19 = bf16[1,2,32,1536]{3,2,1,0:T(8,128)(2,1)} copy(bf16[1,2,32,1536]{3,2,1,0:T(8,128)(2,1)S(1)} %copy-done) | data formatting | bytes 393216
  44.8 0.0 copy-done.1
  44.9 0.6 %copy.20 = f32[8,12]{1,0:T(8,128)} copy(f32[8,12]{1,0:T(8,128)S(1)} %copy-done.1) | data formatting | bytes 768
Async XLA Ops:
  41.8 2.4 %copy-start = (bf16[1,2,32,1536]{3,2,1,0:T(8,128)(2,1)S(1)}, bf16[1,2,32,1536]{3,2,1,0:T(8,128)(2,1)}, u32[]{:S(2)}) copy-start(bf16[1,2,32,1536]{3,2,1,0:T(8,128)(2,1)} %get-tuple-element.7) | copy-start | bytes 589828
  41.8 3.1 %copy-start.1 = (f32[8,12]{1,0:T(8,128)S(1)}, f32[8,12]{1,0:T(8,128)}, u32[]{:S(2)}) copy-start(f32[8,12]{1,0:T(8,128)} %get-tuple-element.8) | copy-start | bytes 1156
